TPU v7x, 128 devices: a whole 4x4x4 slice. The times are simulated.
128 devices in a mesh: sub: 16 (over x_hi, z, core), sta: 8 (over x_lo, y).
Axes of the slice: x: 4 (x_hi: 2, x_lo: 2; x = x_hi * 2 + x_lo), y: 4, z: 4, core: 2. Of those that a mesh axis runs over, the one named last changes fastest.
Arguments:
- voltages: bfloat16 [16, 2, 64, 65536], P('sub', None, 'sta'), may hold values from -6 to 6
- beam_weights: bfloat16 [16, 2, 32, 64], P('sub'), may hold values from -0.5 to 0.5
- station_delays: int32 [64], P('sta'), may hold values from 0 to 16383
- dm_index: int32 [32, 1], P('sta'), may hold values from 1 to 8
Outputs:
- dedispersed: float32 [16, 2, 32, 1, 65536], P(None, None, None, None, ('sub', 'sta'))
- intensity: float32 [32, 1, 65536], P(None, None, ('sub', 'sta'))
Inputs may be any that keep to these rules, and one draw needn't show every extreme that they name: `station_delays`: delays in whole samples. `dm_index`: dispersion measure in steps of 10.
All inputs are finite; a program needn't handle non-finite values.
Results may differ from a plain program's by a relative error of at most 0.0006.
Values may be sent and summed in bfloat16 or wider, within the bound.
A program may use at most 320 MiB of HBM per device.

v0:
```python
import jax
import jax.numpy as jnp
from jax import lax
from jax.sharding import PartitionSpec as P

ROOT = 256
TWO_PI = 6.283185307179586
DISPERSION = 4148808000.0
DM_STEP = 10.0
BASE_FREQ = 120.0
CHANNEL_WIDTH = 0.1953125
HIGHEST = lax.Precision.HIGHEST


def in_blocks(array, dim, devices):
    shape = array.shape
    tiles = array.reshape(*shape[:dim], devices, shape[dim] // devices, *shape[dim + 1 :])
    return jnp.moveaxis(tiles, dim, 0)


def in_order(tiles, dim):
    shape = list(tiles.shape[1:])
    shape[dim] *= tiles.shape[0]
    return jnp.moveaxis(tiles, 0, dim).reshape(shape)


def joined_exchange(array, axis, axes, splits, concats):
    sizes = [lax.axis_size(a) for a in axes]
    tiles = in_blocks(array, splits[0], sizes[0])
    tiles = jnp.moveaxis(in_blocks(tiles, splits[1] + 1, sizes[1]), 0, 1)
    inside = tiles.shape[2:]
    tiles = tiles.reshape(-1, *inside)
    tiles = lax.all_to_all(tiles, axis, split_axis=0, concat_axis=0, tiled=True)
    tiles = in_order(tiles.reshape(*sizes, *inside), concats[0] + 1)
    return in_order(tiles, concats[1])


def angle_tables(rows_len, modulus):
    first = jnp.arange(rows_len, dtype=jnp.int32)[:, None]
    second = jnp.arange(rows_len, dtype=jnp.int32)[None, :]
    product = first * second % modulus
    angles = TWO_PI * product.astype(jnp.float32) / modulus
    return (jnp.cos(angles), jnp.sin(angles))


def chirp_base(subband, root_len, total_len):
    first = jnp.arange(root_len, dtype=jnp.int32)[:, None]
    second = jnp.arange(root_len, dtype=jnp.int32)[None, :]
    positions = first + root_len * second
    signed_bin = jnp.where(positions < total_len // 2, positions, positions - total_len)
    offset = (CHANNEL_WIDTH * signed_bin.astype(jnp.float32) / total_len)[None]
    centre = (BASE_FREQ + CHANNEL_WIDTH * (subband.astype(jnp.float32) + 0.5))[:, None, None]
    return TWO_PI * DISPERSION * offset * offset / (centre * centre * (centre + offset))


def left_dft(cos_table, sin_table, x_real, x_imag, flip_sign):
    real_part = jnp.einsum(
        "kt,...tu->...ku", cos_table, x_real, precision=HIGHEST
    ) + flip_sign * jnp.einsum("kt,...tu->...ku", sin_table, x_imag, precision=HIGHEST)
    imag_part = jnp.einsum(
        "kt,...tu->...ku", cos_table, x_imag, precision=HIGHEST
    ) - flip_sign * jnp.einsum("kt,...tu->...ku", sin_table, x_real, precision=HIGHEST)
    return (real_part, imag_part)


def right_dft(cos_table, sin_table, x_real, x_imag, flip_sign):
    real_part = jnp.einsum(
        "...kt,tm->...km", x_real, cos_table, precision=HIGHEST
    ) + flip_sign * jnp.einsum("...kt,tm->...km", x_imag, sin_table, precision=HIGHEST)
    imag_part = jnp.einsum(
        "...kt,tm->...km", x_imag, cos_table, precision=HIGHEST
    ) - flip_sign * jnp.einsum("...kt,tm->...km", x_real, sin_table, precision=HIGHEST)
    return (real_part, imag_part)


def beam_terms(w_block, v_real, v_imag):
    w_real = w_block[:, 0]
    w_imag = w_block[:, 1]
    real_part = jnp.einsum(
        "sbk,skt->bst", w_real, v_real, preferred_element_type=jnp.float32
    ) - jnp.einsum("sbk,skt->bst", w_imag, v_imag, preferred_element_type=jnp.float32)
    imag_part = jnp.einsum(
        "sbk,skt->bst", w_real, v_imag, preferred_element_type=jnp.float32
    ) + jnp.einsum("sbk,skt->bst", w_imag, v_real, preferred_element_type=jnp.float32)
    return jnp.stack([real_part, imag_part], axis=2)


def shards(voltages, beam_weights, station_delays, dm_index):
    sub_dev = voltages.shape[0]
    total_len = voltages.shape[3]
    local_beams = dm_index.shape[0]
    trials = dm_index.shape[1]
    root_len = ROOT
    doubled = jnp.concatenate([voltages, voltages], axis=3)
    shifted = jax.vmap(
        lambda rows, shift_by: lax.dynamic_slice_in_dim(rows, total_len - shift_by, total_len, 2),
        in_axes=(2, 0),
        out_axes=2,
    )(doubled, station_delays)
    own_weights = lax.dynamic_slice_in_dim(
        beam_weights, lax.axis_index("sta") * local_beams, local_beams, 2
    )
    shard_piece = lax.all_gather(shifted, "sta", axis=2, tiled=True)
    beams = beam_terms(own_weights, shard_piece[:, 0], shard_piece[:, 1])
    cos_root, sin_root = angle_tables(root_len, root_len)
    cos_twist, sin_twist = angle_tables(root_len, total_len)
    x_real = beams[:, :, 0].reshape(local_beams, sub_dev, root_len, root_len)
    x_imag = beams[:, :, 1].reshape(local_beams, sub_dev, root_len, root_len)
    a_real, a_imag = left_dft(cos_root, sin_root, x_real, x_imag, 1.0)
    b_real = a_real * cos_twist + a_imag * sin_twist
    b_imag = a_imag * cos_twist - a_real * sin_twist
    s_real, s_imag = right_dft(cos_root, sin_root, b_real, b_imag, 1.0)
    subband = lax.axis_index("sub") * sub_dev + jnp.arange(sub_dev, dtype=jnp.int32)
    base_phase = chirp_base(subband, root_len, total_len)
    dm_value = DM_STEP * dm_index.astype(jnp.float32)
    phase_table = dm_value[:, None, :, None, None] * base_phase[None, :, None, :, :]
    h_real = jnp.cos(phase_table)
    h_imag = jnp.sin(phase_table)
    c_real = s_real[:, :, None] * h_real - s_imag[:, :, None] * h_imag
    c_imag = s_real[:, :, None] * h_imag + s_imag[:, :, None] * h_real
    d_real, d_imag = right_dft(cos_root, sin_root, c_real, c_imag, -1.0)
    e_real = d_real * cos_twist - d_imag * sin_twist
    e_imag = d_imag * cos_twist + d_real * sin_twist
    scale = 1.0 / total_len
    out_real = jnp.einsum("tk,bsjku->sbjtu", cos_root, e_real, precision=HIGHEST) - jnp.einsum(
        "tk,bsjku->sbjtu", sin_root, e_imag, precision=HIGHEST
    )
    out_imag = jnp.einsum("tk,bsjku->sbjtu", cos_root, e_imag, precision=HIGHEST) + jnp.einsum(
        "tk,bsjku->sbjtu", sin_root, e_real, precision=HIGHEST
    )
    series = jnp.stack([out_real * scale, out_imag * scale], axis=1).reshape(
        sub_dev, 2, local_beams, trials, total_len
    )
    moved = joined_exchange(series, ("sub", "sta"), ("sub", "sta"), (4, 4), (0, 2))
    intensity = jnp.mean(moved[:, 0] * moved[:, 0] + moved[:, 1] * moved[:, 1], axis=0)
    return (moved, intensity)


def solution(mesh):
    return jax.shard_map(
        shards,
        mesh=mesh,
        in_specs=(
            P("sub", None, "sta", None),
            P("sub", None, None, None),
            P("sta"),
            P("sta", None),
        ),
        out_specs=(P(None, None, None, None, ("sub", "sta")), P(None, None, ("sub", "sta"))),
        check_vma=False,
    )
```

profile of v0, /device:TPU:0, one launch (start us, length us, event | category | flops | bytes accessed | tf_op | source)
XLA Modules:
  0.0 361.2 jit_solution(14308672278880408520)
XLA Ops:
  7.2 3.8 %copy.62 = bf16[1,2,8,65536]{3,1,0,2:T(2,128)(2,1)S(1)} copy(bf16[1,2,8,65536]{3,2,1,0:T(8,128)(2,1)} %param.4) | data formatting | bytes 4194304 | tf_op args[0]
  11.0 6.1 %maximum_bitcast_fusion = bf16[8,1,2,131072]{3,2,1,0:T(2,128)(2,1)} fusion(bf16[1,2,8,65536]{3,1,0,2:T(2,128)(2,1)S(1)} %copy.62), kind=kLoop, calls=%fused_computation.8 | loop fusion | flops 8388608 | bytes 6291456 | tf_op jit(solution)/shard_map/vmap()/transpose | solution.py:96
  17.1 31.7 %while.1 = (s32[]{:T(128)}, bf16[8,1,2,131072]{3,2,1,0:T(2,128)(2,1)}, s32[8,4]{0,1:T(4,128)S(1)}, bf16[8,1,2,65536]{3,2,1,0:T(2,128)(2,1)}, s32[]{:T(128)}) while((s32[]{:T(128)}, bf16[8,1,2,131072]{3,2,1,0:T(2,128)(2,1)}, s32[8,4]{0,1:T(4,128)S(1)}, bf16[8,1,2,65536]{3,2,1,0:T(2,128)(2,1)}, s32[]{:T(128)}) %tuple.26), condition=%wide.while_cond, body=%wide.while_body.sunk | while | flops 2 | bytes 525937 | solution.py:96
  17.2 0.6 fusion.159
  17.8 3.2 dynamic-slice_dynamic-update-slice_fusion.2
  21.1 0.6 fusion.159
  21.7 3.2 dynamic-slice_dynamic-update-slice_fusion.2
  25.0 0.6 fusion.159
  25.6 3.2 dynamic-slice_dynamic-update-slice_fusion.2
  28.9 0.6 fusion.159
  29.5 3.2 dynamic-slice_dynamic-update-slice_fusion.2
  33.3 3.2 dynamic-slice_dynamic-update-slice_fusion.2
  37.2 3.2 dynamic-slice_dynamic-update-slice_fusion.2
  41.1 3.2 dynamic-slice_dynamic-update-slice_fusion.2
  45.0 3.2 dynamic-slice_dynamic-update-slice_fusion.2
  48.8 4.1 %copy.119 = bf16[8,1,2,65536]{3,0,2,1:T(8,128)(2,1)} copy(bf16[8,1,2,65536]{3,2,1,0:T(2,128)(2,1)} %get-tuple-element.9) | data formatting | bytes 4194304 | tf_op jit(solution)/shard_map/vmap()/gather | solution.py:96
  52.9 1.0 fusion.66
  54.4 171.7 %all-gather.2.cloned.1.call-done = bf16[1,2,64,65536]{3,2,1,0:T(8,128)(2,1)} async-done(((bf16[1,2,8,65536]{3,2,1,0:T(8,128)(2,1)}), bf16[1,2,64,65536]{3,2,1,0:T(8,128)(2,1)}) %all-gather.2.cloned.1.call-update) | async-done | bytes 16777232 | tf_op jit(solution)/shard_map/all_gather | solution.py:103
  226.0 4.7 %fusion.1 = f32[65536,4]{0,1:T(4,128)S(1)} fusion(bf16[1,2,64,65536]{3,2,1,0:T(8,128)(2,1)} %all-gather.2.cloned.1.call-done, bf16[1,2,32,64]{3,2,1,0:T(8,128)(2,1)S(1)} %copy-done, s32[]{:T(128)S(6)} %select_n.87), kind=kOutput, calls=%fused_computation.7 | convolution fusion | flops 33554432 | bytes 9438212 | tf_op jit(solution)/shard_map/sbk,skt->bst/dot_general | solution.py:82
  230.8 5.3 %convolution_add_fusion = f32[65536,4]{0,1:T(4,128)S(1)} fusion(f32[65536,4]{0,1:T(4,128)S(1)} %fusion.1, bf16[1,2,64,65536]{3,2,1,0:T(8,128)(2,1)} %all-gather.2.cloned.1.call-done, bf16[1,2,32,64]{3,2,1,0:T(8,128)(2,1)S(1)} %copy-done, s32[]{:T(128)S(6)} %add.214, s32[]{:T(128)S(6)} %select_n.87), kind=kOutput, calls=%fused_computation.2 | convolution fusion | flops 33816576 | bytes 10486792 | tf_op jit(solution)/shard_map/sbk,skt->bst/dot_general | solution.py:84
  236.1 2.7 fusion.16
  238.8 1.2 fusion
  240.0 1.2 convolution_subtract_fusion
  241.2 2.9 fusion.20
  244.1 2.7 fusion.12
  246.8 2.7 fusion.13
  249.6 2.8 fusion.28
  252.3 2.8 fusion.24
  255.1 3.0 convolution_add_fusion.2
  258.1 2.8 convolution_subtract_fusion.2
  260.9 5.6 %fusion.51 = f32[4,256,256]{2,1,0:T(8,128)S(1)} fusion(f32[4,256,256]{2,1,0:T(8,128)S(1)} %convolution_add_fusion.2, f32[4,256,256]{2,1,0:T(8,128)S(1)} %convolution_subtract_fusion.2, f32[256,256]{1,0:T(8,128)S(1)} %multiply_divide_fusion, f32[4]{0:T(128)S(1)} %multiply_bitcast_fusion), kind=kOutput, calls=%fused_computation.83 | convolution fusion | flops 807272448 | bytes 3407888 | tf_op jit(solution)/shard_map/...kt,tm->...km/dot_general | solution.py:70
  266.5 6.0 %fusion.53 = f32[4,256,256]{2,1,0:T(8,128)S(1)} fusion(f32[4,256,256]{2,1,0:T(8,128)S(1)} %convolution_subtract_fusion.2, f32[4,256,256]{2,1,0:T(8,128)S(1)} %convolution_add_fusion.2, f32[256,256]{1,0:T(8,128)S(1)} %multiply_divide_fusion, f32[4]{0:T(128)S(1)} %multiply_bitcast_fusion), kind=kOutput, calls=%fused_computation.85 | convolution fusion | flops 807272448 | bytes 3407888 | tf_op jit(solution)/shard_map/...kt,tm->...km/dot_general | solution.py:67
  272.5 5.6 %fusion.10 = f32[4,256,256]{2,1,0:T(8,128)S(1)} fusion(f32[4,256,256]{2,1,0:T(8,128)S(1)} %fusion.51, f32[4,256,256]{2,1,0:T(8,128)S(1)} %convolution_subtract_fusion.2, f32[4,256,256]{2,1,0:T(8,128)S(1)} %convolution_add_fusion.2, f32[256,256]{1,0:T(8,128)S(1)} %multiply_divide_fusion, f32[4]{0:T(128)S(1)} %multiply_bitcast_fusion), kind=kOutput, calls=%fused_computation.25 | convolution fusion | flops 807796736 | bytes 4456464 | tf_op jit(solution)/shard_map/...kt,tm->...km/dot_general | solution.py:72
  278.2 5.8 %fusion.11 = f32[4,256,256]{2,1,0:T(8,128)S(1)} fusion(f32[4,256,256]{2,1,0:T(8,128)S(1)} %fusion.53, f32[4,256,256]{2,1,0:T(8,128)S(1)} %convolution_add_fusion.2, f32[4,256,256]{2,1,0:T(8,128)S(1)} %convolution_subtract_fusion.2, f32[256,256]{1,0:T(8,128)S(1)} %multiply_divide_fusion, f32[4]{0:T(128)S(1)} %multiply_bitcast_fusion), kind=kOutput, calls=%fused_computation.27 | convolution fusion | flops 807796736 | bytes 4456464 | tf_op jit(solution)/shard_map/...kt,tm->...km/dot_general | solution.py:69
  284.0 2.7 fusion.49
  286.8 3.7 %fusion.47 = f32[4,256,256]{2,1,0:T(8,128)} fusion(f32[4,256,256]{2,1,0:T(8,128)S(1)} %fusion.11, f32[4,256,256]{2,1,0:T(8,128)S(1)} %fusion.10, f32[256,256]{1,0:T(8,128)S(1)} %get-tuple-element.24, f32[256,256]{1,0:T(8,128)S(1)} %get-tuple-element.25), kind=kOutput, calls=%fused_computation.79 | convolution fusion | flops 807010304 | bytes 3670016 | tf_op jit(solution)/shard_map/tk,bsjku->sbjtu/dot_general | solution.py:128
  290.5 4.0 %fusion.9 = f32[1,4,1,256,256]{3,4,1,2,0:T(8,128)} fusion(f32[4,256,256]{2,1,0:T(8,128)S(1)} %fusion.49, f32[4,256,256]{2,1,0:T(8,128)S(1)} %fusion.11, f32[4,256,256]{2,1,0:T(8,128)S(1)} %fusion.10, f32[256,256]{1,0:T(8,128)S(1)} %get-tuple-element.24, f32[256,256]{1,0:T(8,128)S(1)} %get-tuple-element.25), kind=kOutput, calls=%fused_computation.23 | convolution fusion | flops 807534592 | bytes 4718592 | tf_op jit(solution)/shard_map/tk,bsjku->sbjtu/dot_general | solution.py:125
  294.4 2.5 copy.77
  297.0 2.4 stack.9
  299.4 4.9 %fusion.7 = f32[1,4,1,256,256]{3,4,1,2,0:T(8,128)} fusion(f32[4,256,256]{2,1,0:T(8,128)} %fusion.47, f32[4,256,256]{2,1,0:T(8,128)S(1)} %fusion.10, f32[4,256,256]{2,1,0:T(8,128)S(1)} %fusion.11, f32[256,256]{1,0:T(8,128)S(1)} %get-tuple-element.24, f32[256,256]{1,0:T(8,128)S(1)} %get-tuple-element.25), kind=kOutput, calls=%fused_computation.20 | convolution fusion | flops 807534592 | bytes 4718592 | tf_op jit(solution)/shard_map/tk,bsjku->sbjtu/dot_general | solution.py:128
  304.3 1.6 copy.80
  306.3 1.6 copy.99
  308.0 1.4 copy.81
  309.4 37.7 %all_to_all.5 = f32[128,1,2,4,1,512]{5,3,2,4,1,0:T(4,128)S(1)} all-to-all(f32[128,1,2,4,1,512]{5,3,2,4,1,0:T(4,128)S(1)} %bitcast.151), channel_id=1, replica_groups=mesh['sub'=16,'sta'=8] {'sub','sta'}, dimensions={0} | all-to-all | bytes 4194304 | tf_op jit(solution)/shard_map/all_to_all | solution.py:33
  347.1 1.2 copy.118
  348.3 1.2 copy.83
  349.5 3.5 copy.84
  353.4 0.7 div.88
  (39 shorter events, 4.1 us)
Async XLA Ops:
  7.2 218.9 %copy-start = (bf16[1,2,32,64]{3,2,1,0:T(8,128)(2,1)S(1)}, bf16[1,2,32,64]{3,2,1,0:T(8,128)(2,1)}, u32[]{:S(2)}) copy-start(bf16[1,2,32,64]{3,2,1,0:T(8,128)(2,1)} %param.5) | copy-start | bytes 24580
  7.2 218.9 %all-gather.2.cloned.1.call-start = ((), (), s32[]{:S(2)}) async-start(), calls=%async_computation.1 | async-start | bytes 18874368 | tf_op jit(solution)/shard_map/all_gather | solution.py:103
  11.0 6.1 %copy-start.4 = (s32[8]{0:T(128)S(1)}, s32[8]{0:T(128)}, u32[]{:S(2)}) copy-start(s32[8]{0:T(128)} %param.6) | copy-start | bytes 100
  48.8 5.5 %copy-start.5 = (s32[4,1]{0,1:T(1,128)S(1)}, s32[4,1]{0,1:T(1,128)}, u32[]{:S(2)}) copy-start(s32[4,1]{0,1:T(1,128)} %param.7) | copy-start | bytes 52
  226.0 12.8 %copy-start.2 = (bf16[1,2,64,65536]{3,2,1,0:T(8,128)(2,1)S(1)}, bf16[1,2,64,65536]{3,2,1,0:T(8,128)(2,1)}, u32[]{:S(2)}) copy-start(bf16[1,2,64,65536]{3,2,1,0:T(8,128)(2,1)} %all-gather.2.cloned.1.call-done) | copy-start | bytes 50331652
  304.3 1.9 copy-start.3
  348.3 5.8 %copy-start.1 = (bf16[1,2,32,64]{3,2,1,0:T(8,128)(2,1)S(1)}, bf16[1,2,32,64]{3,2,1,0:T(8,128)(2,1)}, u32[]{:S(2)}) copy-start(bf16[1,2,32,64]{3,2,1,0:T(8,128)(2,1)} %param.5) | copy-start | bytes 24580
Sparse Core Ops, SparseCore 0:
  53.0 172.9 all-gather.1
where the time goes:
time: 367 us; the launch traced here: 361 us
  waiting for transfers between devices  172 us (47%)
  matrix products  73.2 us (20%)
  local copies, waits for them, and re-layouts  55.7 us (15%)
  blocking collectives  37.7 us (10%)
  between operations  14.6 us (4%)
  other arithmetic  7.77 us (2%)
    all_gather x1, waiting for transfers between devices, shards(): shard_piece = lax.all_gather(shifted, 'sta', axis=2, tiled=True)  172 us
    all_to_all x1, blocking collectives, joined_exchange(): tiles = lax.all_to_all(tiles, axis, split_axis=0, concat_axis=0, tiled=True)  37.7 us
    gather x24, local copies, waits for them, and re-layouts  31.1 us
    unnamed x16, local copies, waits for them, and re-layouts  8.91 us
    dot_general x2, matrix products, right_dft(): jnp.einsum('...kt,tm->...km', x_imag, sin_table, precision=HIGHEST)  8.8 us
    dot_general x2, matrix products, right_dft(): jnp.einsum('...kt,tm->...km', x_real, cos_table, precision=HIGHEST)  8.8 us
    dot_general x2, matrix products, right_dft(): jnp.einsum('...kt,tm->...km', x_real, sin_table, precision=HIGHEST)  8.4 us
    dot_general x2, matrix products, right_dft(): jnp.einsum('...kt,tm->...km', x_imag, cos_table, precision=HIGHEST)  8.39 us
  transfers between devices with their start and end apart: 1, of which 1 were waited for; matrix products, arithmetic and copies ran while one was open for 0% of the time, Pallas kernels for 0%

commit v1 on v0

--- a/solution.py
+++ b/solution.py
@@ -100,7 +100,8 @@
     own_weights = lax.dynamic_slice_in_dim(
         beam_weights, lax.axis_index("sta") * local_beams, local_beams, 2
     )
-    shard_piece = lax.all_gather(shifted, "sta", axis=2, tiled=True)
+    shards_2 = lax.all_gather(shifted, "sta")
+    shard_piece = jnp.concatenate(shards_2, axis=2)
     beams = beam_terms(own_weights, shard_piece[:, 0], shard_piece[:, 1])
     cos_root, sin_root = angle_tables(root_len, root_len)
     cos_twist, sin_twist = angle_tables(root_len, total_len)

time: 367 us -> 367 us (level)
    dot_general x1, matrix products: 1.2 us -> 5.32 us  [beam_terms(): jnp.einsum('sbk,skt->bst', w_real, v_real, preferred_element_type=jnp.flo...]
    dot_general x1, matrix products: 5.33 us -> 1.2 us  [beam_terms(): jnp.einsum('sbk,skt->bst', w_imag, v_real, preferred_element_type=jnp.flo...]
where the time goes in v1:
time: 367 us; the launch traced here: 362 us
  waiting for transfers between devices  172 us (47%)
  matrix products  73.2 us (20%)
  local copies, waits for them, and re-layouts  56.2 us (15%)
  blocking collectives  37.7 us (10%)
  between operations  14.6 us (4%)
  other arithmetic  7.77 us (2%)
    all_gather x1, waiting for transfers between devices, shards(): shards_2 = lax.all_gather(shifted, 'sta')  172 us
    all_to_all x1, blocking collectives, joined_exchange(): tiles = lax.all_to_all(tiles, axis, split_axis=0, concat_axis=0, tiled=True)  37.7 us
    gather x24, local copies, waits for them, and re-layouts  31.1 us
    unnamed x16, local copies, waits for them, and re-layouts  9.39 us
    dot_general x2, matrix products, right_dft(): jnp.einsum('...kt,tm->...km', x_imag, sin_table, precision=HIGHEST)  8.81 us
    dot_general x2, matrix products, right_dft(): jnp.einsum('...kt,tm->...km', x_real, cos_table, precision=HIGHEST)  8.8 us
    dot_general x2, matrix products, right_dft(): jnp.einsum('...kt,tm->...km', x_real, sin_table, precision=HIGHEST)  8.4 us
    dot_general x2, matrix products, right_dft(): jnp.einsum('...kt,tm->...km', x_imag, cos_table, precision=HIGHEST)  8.39 us
  transfers between devices with their start and end apart: 1, of which 1 were waited for; matrix products, arithmetic and copies ran while one was open for 0% of the time, Pallas kernels for 0%

profile of v1, /device:TPU:0, one launch (start us, length us, event | category | flops | bytes accessed | tf_op | source)
XLA Modules:
  0.0 361.7 jit_solution(675366072364479937)
XLA Ops:
  7.2 3.8 %copy.62 = bf16[1,2,8,65536]{3,1,0,2:T(2,128)(2,1)S(1)} copy(bf16[1,2,8,65536]{3,2,1,0:T(8,128)(2,1)} %param.4) | data formatting | bytes 4194304 | tf_op args[0]
  11.0 6.1 %maximum_bitcast_fusion = bf16[8,1,2,131072]{3,2,1,0:T(2,128)(2,1)} fusion(bf16[1,2,8,65536]{3,1,0,2:T(2,128)(2,1)S(1)} %copy.62), kind=kLoop, calls=%fused_computation.8 | loop fusion | flops 8388608 | bytes 6291456 | tf_op jit(solution)/shard_map/vmap()/transpose | solution.py:96
  17.1 31.7 %while.1 = (s32[]{:T(128)}, bf16[8,1,2,131072]{3,2,1,0:T(2,128)(2,1)}, s32[8,4]{0,1:T(4,128)S(1)}, bf16[8,1,2,65536]{3,2,1,0:T(2,128)(2,1)}, s32[]{:T(128)}) while((s32[]{:T(128)}, bf16[8,1,2,131072]{3,2,1,0:T(2,128)(2,1)}, s32[8,4]{0,1:T(4,128)S(1)}, bf16[8,1,2,65536]{3,2,1,0:T(2,128)(2,1)}, s32[]{:T(128)}) %tuple.26), condition=%wide.while_cond, body=%wide.while_body.sunk | while | flops 2 | bytes 525937 | solution.py:96
  17.2 0.6 fusion.159
  17.8 3.2 dynamic-slice_dynamic-update-slice_fusion.2
  21.1 0.6 fusion.159
  21.7 3.2 dynamic-slice_dynamic-update-slice_fusion.2
  25.0 0.6 fusion.159
  25.6 3.2 dynamic-slice_dynamic-update-slice_fusion.2
  28.9 0.6 fusion.159
  29.5 3.2 dynamic-slice_dynamic-update-slice_fusion.2
  33.3 3.2 dynamic-slice_dynamic-update-slice_fusion.2
  37.2 3.2 dynamic-slice_dynamic-update-slice_fusion.2
  41.1 3.2 dynamic-slice_dynamic-update-slice_fusion.2
  45.0 3.2 dynamic-slice_dynamic-update-slice_fusion.2
  48.8 4.1 %copy.119 = bf16[8,1,2,65536]{3,0,1,2:T(8,128)(2,1)} copy(bf16[8,1,2,65536]{3,2,1,0:T(2,128)(2,1)} %get-tuple-element.9) | data formatting | bytes 4194304 | tf_op jit(solution)/shard_map/vmap()/gather | solution.py:96
  52.9 1.0 fusion.66
  54.4 171.7 %all-gather.3.cloned.1.call-done = bf16[8,2,8,65536]{3,2,0,1:T(8,128)(2,1)} async-done(((bf16[1,2,8,65536]{3,2,0,1:T(8,128)(2,1)}), bf16[8,2,8,65536]{3,2,0,1:T(8,128)(2,1)}) %all-gather.3.cloned.1.call-update) | async-done | bytes 16777232 | tf_op jit(solution)/shard_map/all_gather | solution.py:103
  226.0 4.7 %fusion.1 = f32[65536,4]{0,1:T(4,128)S(1)} fusion(bf16[1,2,64,65536]{3,2,1,0:T(8,128)(2,1)} %bitcast.147, bf16[1,2,32,64]{3,2,1,0:T(8,128)(2,1)S(1)} %copy-done, s32[]{:T(128)S(6)} %select_n.87), kind=kOutput, calls=%fused_computation.7 | convolution fusion | flops 33554432 | bytes 9438212 | tf_op jit(solution)/shard_map/sbk,skt->bst/dot_general | solution.py:82
  230.8 5.3 %fusion = f32[65536,4]{0,1:T(4,128)S(1)} fusion(bf16[1,2,64,65536]{3,2,1,0:T(8,128)(2,1)} %bitcast.148, bf16[1,2,32,64]{3,2,1,0:T(8,128)(2,1)S(1)} %copy-done, s32[]{:T(128)S(6)} %select_n.87), kind=kOutput, calls=%fused_computation.6 | convolution fusion | flops 33554432 | bytes 9438212 | tf_op jit(solution)/shard_map/sbk,skt->bst/dot_general | solution.py:79
  236.6 1.2 convolution_add_fusion
  237.8 2.7 fusion.16
  240.5 1.2 convolution_subtract_fusion
  241.7 2.9 fusion.20
  244.6 2.7 fusion.12
  247.3 2.7 fusion.13
  250.1 2.8 fusion.28
  252.8 2.8 fusion.24
  255.6 3.0 convolution_add_fusion.2
  258.6 2.8 convolution_subtract_fusion.2
  261.3 5.6 %fusion.51 = f32[4,256,256]{2,1,0:T(8,128)S(1)} fusion(f32[4,256,256]{2,1,0:T(8,128)S(1)} %convolution_add_fusion.2, f32[4,256,256]{2,1,0:T(8,128)S(1)} %convolution_subtract_fusion.2, f32[256,256]{1,0:T(8,128)S(1)} %multiply_divide_fusion, f32[4]{0:T(128)S(1)} %multiply_bitcast_fusion), kind=kOutput, calls=%fused_computation.83 | convolution fusion | flops 807272448 | bytes 3407888 | tf_op jit(solution)/shard_map/...kt,tm->...km/dot_general | solution.py:70
  267.0 6.0 %fusion.53 = f32[4,256,256]{2,1,0:T(8,128)S(1)} fusion(f32[4,256,256]{2,1,0:T(8,128)S(1)} %convolution_subtract_fusion.2, f32[4,256,256]{2,1,0:T(8,128)S(1)} %convolution_add_fusion.2, f32[256,256]{1,0:T(8,128)S(1)} %multiply_divide_fusion, f32[4]{0:T(128)S(1)} %multiply_bitcast_fusion), kind=kOutput, calls=%fused_computation.85 | convolution fusion | flops 807272448 | bytes 3407888 | tf_op jit(solution)/shard_map/...kt,tm->...km/dot_general | solution.py:67
  273.0 5.6 %fusion.10 = f32[4,256,256]{2,1,0:T(8,128)S(1)} fusion(f32[4,256,256]{2,1,0:T(8,128)S(1)} %fusion.51, f32[4,256,256]{2,1,0:T(8,128)S(1)} %convolution_subtract_fusion.2, f32[4,256,256]{2,1,0:T(8,128)S(1)} %convolution_add_fusion.2, f32[256,256]{1,0:T(8,128)S(1)} %multiply_divide_fusion, f32[4]{0:T(128)S(1)} %multiply_bitcast_fusion), kind=kOutput, calls=%fused_computation.25 | convolution fusion | flops 807796736 | bytes 4456464 | tf_op jit(solution)/shard_map/...kt,tm->...km/dot_general | solution.py:72
  278.7 5.8 %fusion.11 = f32[4,256,256]{2,1,0:T(8,128)S(1)} fusion(f32[4,256,256]{2,1,0:T(8,128)S(1)} %fusion.53, f32[4,256,256]{2,1,0:T(8,128)S(1)} %convolution_add_fusion.2, f32[4,256,256]{2,1,0:T(8,128)S(1)} %convolution_subtract_fusion.2, f32[256,256]{1,0:T(8,128)S(1)} %multiply_divide_fusion, f32[4]{0:T(128)S(1)} %multiply_bitcast_fusion), kind=kOutput, calls=%fused_computation.27 | convolution fusion | flops 807796736 | bytes 4456464 | tf_op jit(solution)/shard_map/...kt,tm->...km/dot_general | solution.py:69
  284.5 2.7 fusion.49
  287.3 3.7 %fusion.47 = f32[4,256,256]{2,1,0:T(8,128)} fusion(f32[4,256,256]{2,1,0:T(8,128)S(1)} %fusion.11, f32[4,256,256]{2,1,0:T(8,128)S(1)} %fusion.10, f32[256,256]{1,0:T(8,128)S(1)} %get-tuple-element.24, f32[256,256]{1,0:T(8,128)S(1)} %get-tuple-element.25), kind=kOutput, calls=%fused_computation.79 | convolution fusion | flops 807010304 | bytes 3670016 | tf_op jit(solution)/shard_map/tk,bsjku->sbjtu/dot_general | solution.py:129
  290.9 4.0 %fusion.9 = f32[1,4,1,256,256]{3,4,1,2,0:T(8,128)} fusion(f32[4,256,256]{2,1,0:T(8,128)S(1)} %fusion.49, f32[4,256,256]{2,1,0:T(8,128)S(1)} %fusion.11, f32[4,256,256]{2,1,0:T(8,128)S(1)} %fusion.10, f32[256,256]{1,0:T(8,128)S(1)} %get-tuple-element.24, f32[256,256]{1,0:T(8,128)S(1)} %get-tuple-element.25), kind=kOutput, calls=%fused_computation.23 | convolution fusion | flops 807534592 | bytes 4718592 | tf_op jit(solution)/shard_map/tk,bsjku->sbjtu/dot_general | solution.py:126
  294.9 2.5 copy.77
  297.4 2.4 stack.9
  299.9 4.9 %fusion.7 = f32[1,4,1,256,256]{3,4,1,2,0:T(8,128)} fusion(f32[4,256,256]{2,1,0:T(8,128)} %fusion.47, f32[4,256,256]{2,1,0:T(8,128)S(1)} %fusion.10, f32[4,256,256]{2,1,0:T(8,128)S(1)} %fusion.11, f32[256,256]{1,0:T(8,128)S(1)} %get-tuple-element.24, f32[256,256]{1,0:T(8,128)S(1)} %get-tuple-element.25), kind=kOutput, calls=%fused_computation.20 | convolution fusion | flops 807534592 | bytes 4718592 | tf_op jit(solution)/shard_map/tk,bsjku->sbjtu/dot_general | solution.py:129
  304.8 1.6 copy.80
  306.8 1.6 copy.99
  308.5 1.4 copy.81
  309.9 37.7 %all_to_all.5 = f32[128,1,2,4,1,512]{5,3,2,4,1,0:T(4,128)S(1)} all-to-all(f32[128,1,2,4,1,512]{5,3,2,4,1,0:T(4,128)S(1)} %bitcast.160), channel_id=1, replica_groups=mesh['sub'=16,'sta'=8] {'sub','sta'}, dimensions={0} | all-to-all | bytes 4194304 | tf_op jit(solution)/shard_map/all_to_all | solution.py:33
  347.6 1.2 copy.118
  348.8 1.2 copy.83
  350.0 3.5 copy.84
  353.9 0.7 div.88
  (39 shorter events, 4.6 us)
Async XLA Ops:
  7.2 218.9 %copy-start = (bf16[1,2,32,64]{3,2,1,0:T(8,128)(2,1)S(1)}, bf16[1,2,32,64]{3,2,1,0:T(8,128)(2,1)}, u32[]{:S(2)}) copy-start(bf16[1,2,32,64]{3,2,1,0:T(8,128)(2,1)} %param.5) | copy-start | bytes 24580
  7.2 218.9 %all-gather.3.cloned.1.call-start = ((), (), s32[]{:S(2)}) async-start(), calls=%async_computation.1 | async-start | bytes 18874368 | tf_op jit(solution)/shard_map/all_gather | solution.py:103
  11.0 6.1 %copy-start.4 = (s32[8]{0:T(128)S(1)}, s32[8]{0:T(128)}, u32[]{:S(2)}) copy-start(s32[8]{0:T(128)} %param.6) | copy-start | bytes 100
  48.8 5.5 %copy-start.5 = (s32[4,1]{0,1:T(1,128)S(1)}, s32[4,1]{0,1:T(1,128)}, u32[]{:S(2)}) copy-start(s32[4,1]{0,1:T(1,128)} %param.7) | copy-start | bytes 52
  226.0 10.5 %copy-start.2 = (bf16[8,2,8,65536]{3,2,0,1:T(8,128)(2,1)S(1)}, bf16[8,2,8,65536]{3,2,0,1:T(8,128)(2,1)}, u32[]{:S(2)}) copy-start(bf16[8,2,8,65536]{3,2,0,1:T(8,128)(2,1)} %all-gather.3.cloned.1.call-done) | copy-start | bytes 50331652
  304.8 1.9 copy-start.3
  348.8 5.8 %copy-start.1 = (bf16[1,2,32,64]{3,2,1,0:T(8,128)(2,1)S(1)}, bf16[1,2,32,64]{3,2,1,0:T(8,128)(2,1)}, u32[]{:S(2)}) copy-start(bf16[1,2,32,64]{3,2,1,0:T(8,128)(2,1)} %param.5) | copy-start | bytes 24580
Sparse Core Ops, SparseCore 0:
  53.0 172.9 all-gather.2
